TPU v7x, 8 devices: a whole 2x2x1 slice. The times are simulated.
8 devices in a mesh: depth: 2 (over z, y), col: 2 (over x), row: 2 (over core).
Axes of the slice: x: 2, y: 2, z: 1, core: 2. Of those that a mesh axis runs over, the one named last changes fastest.
Arguments:
- reach_in: bfloat16 [5120, 5120], P(('row', 'depth'), 'col')
Outputs:
- output: bfloat16 [5120, 5120], P(('row', 'depth'), 'col')
All inputs are finite; a program needn't handle non-finite values.
Results may differ from a plain program's by a relative error of at most 0.001.
Values are sent between devices in bfloat16 or wider.
A program may use at most 1 GiB of HBM per device.

v0:
```python
import jax
import jax.numpy as jnp
from jax import lax
from jax.sharding import PartitionSpec as P

SQUARINGS = 4


def solution(mesh):
    depth_size = mesh.shape['depth']
    col_size = mesh.shape['col']
    row_size = mesh.shape['row']
    col_ratio = row_size // col_size
    per_layer = row_size // depth_size
    n_used = min(col_ratio, per_layer)
    all_axes = ('depth', 'col', 'row')

    def linear(layer_id, col_id, row_id):
        return (layer_id * col_size + col_id) * row_size + row_id

    def a_perm(piece_id):
        perm_pairs = []
        for layer_id in range(depth_size):
            for col_id in range(col_size):
                for row_id in range(row_size):
                    offset = (row_id + layer_id * per_layer + piece_id) // col_ratio
                    perm_pairs.append((linear(layer_id, col_id, row_id), linear(layer_id, (col_id - offset) % col_size, row_id)))
        return perm_pairs

    def b_perm():
        perm_pairs = []
        for layer_id in range(depth_size):
            for col_id in range(col_size):
                for k_id in range(row_size):
                    dest_row = (k_id - col_id * col_ratio - layer_id * per_layer) % row_size
                    perm_pairs.append((linear(layer_id, col_id, k_id), linear(layer_id, col_id, dest_row)))
        return perm_pairs

    a_perms = [a_perm(piece_id) for piece_id in range(n_used)]
    b_skew = b_perm()
    col_shift = [(col_id, (col_id - 1) % col_size) for col_id in range(col_size)]
    row_shift = [(row_id, (row_id - 1) % row_size) for row_id in range(row_size)]

    def local_squarings(row_slab):
        row_idx = lax.axis_index('row')
        layer_idx = lax.axis_index('depth')
        for _ in range(SQUARINGS):
            full_block = lax.all_gather(row_slab, 'depth', axis=0, tiled=True)
            k_width = full_block.shape[0]
            window = []
            for piece_id in range(n_used):
                if col_ratio == 1:
                    a_piece = full_block
                else:
                    sub_idx = (row_idx + layer_idx * per_layer + piece_id) % col_ratio
                    a_piece = lax.dynamic_slice_in_dim(full_block, sub_idx * k_width, k_width, axis=1)
                window.append(lax.ppermute(a_piece, all_axes, a_perms[piece_id]))
            b_block = lax.ppermute(full_block, all_axes, b_skew)
            partial_sum = None
            for step_id in range(per_layer):
                slot_id = step_id % col_ratio
                product = jnp.dot(window[slot_id], b_block, preferred_element_type=jnp.float32)
                partial_sum = product if partial_sum is None else partial_sum + product
                if step_id + col_ratio < per_layer:
                    window[slot_id] = lax.ppermute(window[slot_id], 'col', col_shift)
                if step_id + 1 < per_layer:
                    b_block = lax.ppermute(b_block, 'row', row_shift)
            reduced = lax.psum_scatter(partial_sum, 'depth', scatter_dimension=0, tiled=True)
            row_slab = jnp.minimum(reduced + row_slab.astype(jnp.float32), 1.0).astype(jnp.bfloat16)
        return row_slab

    layout = P(('row', 'depth'), 'col')
    return jax.shard_map(local_squarings, mesh=mesh, in_specs=(layout,), out_specs=layout, check_vma=False)
```

profile of v0, /device:TPU:0, one launch (start us, length us, event | category | flops | bytes accessed | tf_op | source)
XLA Modules:
  0.0 2599.3 jit_solution(3036244028499025435)
XLA Ops:
  6.5 0.0 all-gather.5.cloned.1.call-start
  6.5 0.7 all-gather.5.cloned.1.call-update
  7.3 0.0 reduce-scatter.5.cloned.1.call-start
  7.3 160.7 %all-gather.5.cloned.1.call-done = bf16[2560,2560]{1,0:T(8,128)(2,1)} async-done(((bf16[1280,2560]{1,0:T(8,128)(2,1)}), bf16[2560,2560]{1,0:T(8,128)(2,1)}) %all-gather.5.cloned.1.call-update) | async-done | bytes 13107216 | tf_op jit(solution)/shard_map/all_gather | solution.py:48
  168.0 5.4 collective-permute-start.1
  173.4 99.7 %collective-permute-start = (bf16[2560,2560]{1,0:T(8,128)(2,1)}, bf16[2560,2560]{1,0:T(8,128)(2,1)}, u32[]{:S(2)}, u32[]{:S(2)}) collective-permute-start(bf16[2560,2560]{1,0:T(8,128)(2,1)} %all-gather.5.cloned.1.call-done), channel_id=1, source_target_pairs={{0,0},{1,3},{2,2},{3,1},{4,6},{5,5},{6,4},{7,7}} | collective-permute-start | bytes 39321608 | tf_op jit(solution)/shard_map/ppermute | solution.py:57
  273.1 0.0 collective-permute-done.1
  273.1 0.0 collective-permute-done
  273.1 39.1 %fusion = f32[2560,2560]{1,0:T(8,128)} fusion(bf16[2560,2560]{1,0:T(8,128)(2,1)} %collective-permute-done, bf16[2560,2560]{1,0:T(8,128)(2,1)S(1)} %collective-permute-done.1), kind=kOutput, calls=%fused_computation.4 | convolution fusion | flops 33554432000 | bytes 52428800 | tf_op jit(solution)/shard_map/dot_general | solution.py:62
  312.2 0.0 reduce-scatter.5.cloned.1.call-update
  312.2 0.0 all-gather.7.cloned.1.call-start
  312.3 334.1 %reduce-scatter.5.cloned.1.call-done = f32[1280,2560]{1,0:T(8,128)} async-done(((f32[2560,2560]{1,0:T(8,128)}), f32[1280,2560]{1,0:T(8,128)}) %reduce-scatter.5.cloned.1.call-update) | async-done | bytes 13107216 | tf_op jit(solution)/shard_map/reduce_scatter | solution.py:68
  646.4 10.4 minimum_convert_fusion.3
  656.8 0.0 all-gather.7.cloned.1.call-update
  656.8 0.0 reduce-scatter.7.cloned.1.call-start
  656.8 156.4 %all-gather.7.cloned.1.call-done = bf16[2560,2560]{1,0:T(8,128)(2,1)} async-done(((bf16[1280,2560]{1,0:T(8,128)(2,1)}), bf16[2560,2560]{1,0:T(8,128)(2,1)}) %all-gather.7.cloned.1.call-update) | async-done | bytes 13107216 | tf_op jit(solution)/shard_map/all_gather | solution.py:48
  813.3 5.4 collective-permute-start.3
  818.6 99.7 %collective-permute-start.2 = (bf16[2560,2560]{1,0:T(8,128)(2,1)}, bf16[2560,2560]{1,0:T(8,128)(2,1)}, u32[]{:S(2)}, u32[]{:S(2)}) collective-permute-start(bf16[2560,2560]{1,0:T(8,128)(2,1)} %all-gather.7.cloned.1.call-done), channel_id=1, source_target_pairs={{0,0},{1,3},{2,2},{3,1},{4,6},{5,5},{6,4},{7,7}} | collective-permute-start | bytes 39321608 | tf_op jit(solution)/shard_map/ppermute | solution.py:57
  918.3 0.0 collective-permute-done.3
  918.3 0.0 collective-permute-done.2
  918.3 39.1 %fusion.1 = f32[2560,2560]{1,0:T(8,128)} fusion(bf16[2560,2560]{1,0:T(8,128)(2,1)} %collective-permute-done.2, bf16[2560,2560]{1,0:T(8,128)(2,1)S(1)} %collective-permute-done.3), kind=kOutput, calls=%fused_computation.5 | convolution fusion | flops 33554432000 | bytes 52428800 | tf_op jit(solution)/shard_map/dot_general | solution.py:62
  957.4 0.0 reduce-scatter.7.cloned.1.call-update
  957.5 0.0 all-gather.9.cloned.1.call-start
  957.5 334.1 %reduce-scatter.7.cloned.1.call-done = f32[1280,2560]{1,0:T(8,128)} async-done(((f32[2560,2560]{1,0:T(8,128)}), f32[1280,2560]{1,0:T(8,128)}) %reduce-scatter.7.cloned.1.call-update) | async-done | bytes 13107216 | tf_op jit(solution)/shard_map/reduce_scatter | solution.py:68
  1291.6 10.4 minimum_convert_fusion.2
  1302.0 0.0 all-gather.9.cloned.1.call-update
  1302.0 0.0 reduce-scatter.9.cloned.1.call-start
  1302.1 156.4 %all-gather.9.cloned.1.call-done = bf16[2560,2560]{1,0:T(8,128)(2,1)} async-done(((bf16[1280,2560]{1,0:T(8,128)(2,1)}), bf16[2560,2560]{1,0:T(8,128)(2,1)}) %all-gather.9.cloned.1.call-update) | async-done | bytes 13107216 | tf_op jit(solution)/shard_map/all_gather | solution.py:48
  1458.5 5.4 collective-permute-start.5
  1463.9 99.7 %collective-permute-start.4 = (bf16[2560,2560]{1,0:T(8,128)(2,1)}, bf16[2560,2560]{1,0:T(8,128)(2,1)}, u32[]{:S(2)}, u32[]{:S(2)}) collective-permute-start(bf16[2560,2560]{1,0:T(8,128)(2,1)} %all-gather.9.cloned.1.call-done), channel_id=1, source_target_pairs={{0,0},{1,3},{2,2},{3,1},{4,6},{5,5},{6,4},{7,7}} | collective-permute-start | bytes 39321608 | tf_op jit(solution)/shard_map/ppermute | solution.py:57
  1563.5 0.0 collective-permute-done.5
  1563.5 0.0 collective-permute-done.4
  1563.5 39.1 %fusion.2 = f32[2560,2560]{1,0:T(8,128)} fusion(bf16[2560,2560]{1,0:T(8,128)(2,1)} %collective-permute-done.4, bf16[2560,2560]{1,0:T(8,128)(2,1)S(1)} %collective-permute-done.5), kind=kOutput, calls=%fused_computation.6 | convolution fusion | flops 33554432000 | bytes 52428800 | tf_op jit(solution)/shard_map/dot_general | solution.py:62
  1602.7 0.0 reduce-scatter.9.cloned.1.call-update
  1602.7 0.0 all-gather.11.cloned.1.call-start
  1602.7 334.1 %reduce-scatter.9.cloned.1.call-done = f32[1280,2560]{1,0:T(8,128)} async-done(((f32[2560,2560]{1,0:T(8,128)}), f32[1280,2560]{1,0:T(8,128)}) %reduce-scatter.9.cloned.1.call-update) | async-done | bytes 13107216 | tf_op jit(solution)/shard_map/reduce_scatter | solution.py:68
  1936.8 10.4 minimum_convert_fusion.1
  1947.2 0.0 all-gather.11.cloned.1.call-update
  1947.2 0.0 reduce-scatter.11.cloned.1.call-start
  1947.3 156.4 %all-gather.11.cloned.1.call-done = bf16[2560,2560]{1,0:T(8,128)(2,1)} async-done(((bf16[1280,2560]{1,0:T(8,128)(2,1)}), bf16[2560,2560]{1,0:T(8,128)(2,1)}) %all-gather.11.cloned.1.call-update) | async-done | bytes 13107216 | tf_op jit(solution)/shard_map/all_gather | solution.py:48
  2103.7 5.4 collective-permute-start.7
  2109.1 99.7 %collective-permute-start.6 = (bf16[2560,2560]{1,0:T(8,128)(2,1)}, bf16[2560,2560]{1,0:T(8,128)(2,1)}, u32[]{:S(2)}, u32[]{:S(2)}) collective-permute-start(bf16[2560,2560]{1,0:T(8,128)(2,1)} %all-gather.11.cloned.1.call-done), channel_id=1, source_target_pairs={{0,0},{1,3},{2,2},{3,1},{4,6},{5,5},{6,4},{7,7}} | collective-permute-start | bytes 39321608 | tf_op jit(solution)/shard_map/ppermute | solution.py:57
  2208.7 0.0 collective-permute-done.7
  2208.7 0.0 collective-permute-done.6
  2208.7 39.1 %fusion.3 = f32[2560,2560]{1,0:T(8,128)} fusion(bf16[2560,2560]{1,0:T(8,128)(2,1)} %collective-permute-done.6, bf16[2560,2560]{1,0:T(8,128)(2,1)S(1)} %collective-permute-done.7), kind=kOutput, calls=%fused_computation.7 | convolution fusion | flops 33554432000 | bytes 52428800 | tf_op jit(solution)/shard_map/dot_general | solution.py:62
  2247.9 0.0 reduce-scatter.11.cloned.1.call-update
  2247.9 334.1 %reduce-scatter.11.cloned.1.call-done = f32[1280,2560]{1,0:T(8,128)} async-done(((f32[2560,2560]{1,0:T(8,128)}), f32[1280,2560]{1,0:T(8,128)}) %reduce-scatter.11.cloned.1.call-update) | async-done | bytes 13107216 | tf_op jit(solution)/shard_map/reduce_scatter | solution.py:68
  2582.0 10.4 minimum_convert_fusion
Async XLA Ops:
  6.5 161.5 %all-gather.5.cloned.1.call-start = ((), (), s32[]{:S(2)}) async-start(), calls=%async_computation.4 | async-start | bytes 19660800 | tf_op jit(solution)/shard_map/all_gather | solution.py:48
  7.3 639.1 %reduce-scatter.5.cloned.1.call-start = ((), (), s32[]{:S(2)}) async-start(), calls=%async_computation.5 | async-start | bytes 39321600 | tf_op jit(solution)/shard_map/reduce_scatter | solution.py:68
  168.0 105.0 %collective-permute-start.1 = (bf16[2560,2560]{1,0:T(8,128)(2,1)}, bf16[2560,2560]{1,0:T(8,128)(2,1)S(1)}, u32[]{:S(2)}, u32[]{:S(2)}) collective-permute-start(bf16[2560,2560]{1,0:T(8,128)(2,1)} %all-gather.5.cloned.1.call-done), channel_id=1, source_target_pairs={{0,0},{1,1},{2,3},{3,2},{4,5},{5,4},{6,6},{7,7}} | collective-permute-start | bytes 39321608 | tf_op jit(solution)/shard_map/ppermute | solution.py:58
  173.4 99.7 %collective-permute-start = (bf16[2560,2560]{1,0:T(8,128)(2,1)}, bf16[2560,2560]{1,0:T(8,128)(2,1)}, u32[]{:S(2)}, u32[]{:S(2)}) collective-permute-start(bf16[2560,2560]{1,0:T(8,128)(2,1)} %all-gather.5.cloned.1.call-done), channel_id=1, source_target_pairs={{0,0},{1,3},{2,2},{3,1},{4,6},{5,5},{6,4},{7,7}} | collective-permute-start | bytes 39321608 | tf_op jit(solution)/shard_map/ppermute | solution.py:57
  312.2 501.0 %all-gather.7.cloned.1.call-start = ((), (), s32[]{:S(2)}) async-start(), calls=%async_computation.6 | async-start | bytes 19660800 | tf_op jit(solution)/shard_map/all_gather | solution.py:48
  656.8 634.8 %reduce-scatter.7.cloned.1.call-start = ((), (), s32[]{:S(2)}) async-start(), calls=%async_computation.7 | async-start | bytes 39321600 | tf_op jit(solution)/shard_map/reduce_scatter | solution.py:68
  813.3 105.0 %collective-permute-start.3 = (bf16[2560,2560]{1,0:T(8,128)(2,1)}, bf16[2560,2560]{1,0:T(8,128)(2,1)S(1)}, u32[]{:S(2)}, u32[]{:S(2)}) collective-permute-start(bf16[2560,2560]{1,0:T(8,128)(2,1)} %all-gather.7.cloned.1.call-done), channel_id=1, source_target_pairs={{0,0},{1,1},{2,3},{3,2},{4,5},{5,4},{6,6},{7,7}} | collective-permute-start | bytes 39321608 | tf_op jit(solution)/shard_map/ppermute | solution.py:58
  818.6 99.7 %collective-permute-start.2 = (bf16[2560,2560]{1,0:T(8,128)(2,1)}, bf16[2560,2560]{1,0:T(8,128)(2,1)}, u32[]{:S(2)}, u32[]{:S(2)}) collective-permute-start(bf16[2560,2560]{1,0:T(8,128)(2,1)} %all-gather.7.cloned.1.call-done), channel_id=1, source_target_pairs={{0,0},{1,3},{2,2},{3,1},{4,6},{5,5},{6,4},{7,7}} | collective-permute-start | bytes 39321608 | tf_op jit(solution)/shard_map/ppermute | solution.py:57
  957.5 501.0 %all-gather.9.cloned.1.call-start = ((), (), s32[]{:S(2)}) async-start(), calls=%async_computation.8 | async-start | bytes 19660800 | tf_op jit(solution)/shard_map/all_gather | solution.py:48
  1302.0 634.8 %reduce-scatter.9.cloned.1.call-start = ((), (), s32[]{:S(2)}) async-start(), calls=%async_computation.9 | async-start | bytes 39321600 | tf_op jit(solution)/shard_map/reduce_scatter | solution.py:68
  1458.5 105.0 %collective-permute-start.5 = (bf16[2560,2560]{1,0:T(8,128)(2,1)}, bf16[2560,2560]{1,0:T(8,128)(2,1)S(1)}, u32[]{:S(2)}, u32[]{:S(2)}) collective-permute-start(bf16[2560,2560]{1,0:T(8,128)(2,1)} %all-gather.9.cloned.1.call-done), channel_id=1, source_target_pairs={{0,0},{1,1},{2,3},{3,2},{4,5},{5,4},{6,6},{7,7}} | collective-permute-start | bytes 39321608 | tf_op jit(solution)/shard_map/ppermute | solution.py:58
  1463.9 99.7 %collective-permute-start.4 = (bf16[2560,2560]{1,0:T(8,128)(2,1)}, bf16[2560,2560]{1,0:T(8,128)(2,1)}, u32[]{:S(2)}, u32[]{:S(2)}) collective-permute-start(bf16[2560,2560]{1,0:T(8,128)(2,1)} %all-gather.9.cloned.1.call-done), channel_id=1, source_target_pairs={{0,0},{1,3},{2,2},{3,1},{4,6},{5,5},{6,4},{7,7}} | collective-permute-start | bytes 39321608 | tf_op jit(solution)/shard_map/ppermute | solution.py:57
  1602.7 501.0 %all-gather.11.cloned.1.call-start = ((), (), s32[]{:S(2)}) async-start(), calls=%async_computation.10 | async-start | bytes 19660800 | tf_op jit(solution)/shard_map/all_gather | solution.py:48
  1947.2 634.8 %reduce-scatter.11.cloned.1.call-start = ((), (), s32[]{:S(2)}) async-start(), calls=%async_computation.11 | async-start | bytes 39321600 | tf_op jit(solution)/shard_map/reduce_scatter | solution.py:68
  2103.7 105.0 %collective-permute-start.7 = (bf16[2560,2560]{1,0:T(8,128)(2,1)}, bf16[2560,2560]{1,0:T(8,128)(2,1)S(1)}, u32[]{:S(2)}, u32[]{:S(2)}) collective-permute-start(bf16[2560,2560]{1,0:T(8,128)(2,1)} %all-gather.11.cloned.1.call-done), channel_id=1, source_target_pairs={{0,0},{1,1},{2,3},{3,2},{4,5},{5,4},{6,6},{7,7}} | collective-permute-start | bytes 39321608 | tf_op jit(solution)/shard_map/ppermute | solution.py:58
  2109.1 99.7 %collective-permute-start.6 = (bf16[2560,2560]{1,0:T(8,128)(2,1)}, bf16[2560,2560]{1,0:T(8,128)(2,1)}, u32[]{:S(2)}, u32[]{:S(2)}) collective-permute-start(bf16[2560,2560]{1,0:T(8,128)(2,1)} %all-gather.11.cloned.1.call-done), channel_id=1, source_target_pairs={{0,0},{1,3},{2,2},{3,1},{4,6},{5,5},{6,4},{7,7}} | collective-permute-start | bytes 39321608 | tf_op jit(solution)/shard_map/ppermute | solution.py:57
Sparse Core Ops, SparseCore 0:
  8.9 159.1 all-gather.4
  312.4 333.9 reduce-scatter.4
  656.9 156.3 all-gather.6
  957.6 333.9 reduce-scatter.6
  1302.1 156.3 all-gather.8
  1602.8 333.9 reduce-scatter.8
  1947.4 156.2 all-gather.10
  2248.0 333.9 reduce-scatter.10
where the time goes:
time: 2630 us; the launch traced here: 2600 us
  waiting for transfers between devices  1970 us (75%)
  starting transfers between devices  420 us (16%)
  matrix products  157 us (6%)
  other arithmetic  41.5 us (2%)
    reduce_scatter x4, waiting for transfers between devices, local_squarings(): lax.psum_scatter(partial_sum, 'depth', scatter_dimension=0, tiled=True)  1340 us
    all_gather x4, waiting for transfers between devices, local_squarings(): full_block = lax.all_gather(row_slab, 'depth', axis=0, tiled=True)  630 us
    ppermute x4, starting transfers between devices, local_squarings(): window.append(lax.ppermute(a_piece, all_axes, a_perms[piece_id]))  399 us
    dot_general x4, matrix products, local_squarings(): jnp.dot(window[slot_id], b_block, preferred_element_type=jnp.float32)  157 us
  transfers between devices with their start and end apart: 16, of which 8 were waited for; matrix products, arithmetic and copies ran while one was open for 0% of the time, Pallas kernels for 0%

commit v1 on v0

v1 whole, which is shorter than its diff:
```python
import functools

import jax
import jax.numpy as jnp
from jax import lax
from jax.experimental import pallas as pl
from jax.experimental.pallas import tpu as pltpu
from jax.sharding import PartitionSpec as P

MESH = pl.DeviceIdType.MESH
NC = 10
SHARE2 = 6
SHARE3 = 5


def kernel(n, s_ref, o_ref, r0, r1, r2, r3, panel, bbuf,
           loc, ps, pr, xs, xr, ys, yr, bsem, osem, rdy):
    half, slab, width = n // 2, n // 4, n // (2 * NC)
    l = lax.axis_index('depth')
    j = lax.axis_index('col')
    i = lax.axis_index('row')
    x_dev, y_dev, p_dev = {'col': 1 - j}, {'depth': 1 - l}, {'row': 1 - i}

    def mo(v, m):
        return pl.multiple_of(v, m)

    def rows(ls):
        return pl.ds(mo(ls * slab, slab), slab)

    def cols(c):
        return pl.ds(mo(c * width, width), width)

    def pv(buf, ls, c):
        return panel.at[buf, rows(ls), cols(c)]

    def rv(r, ls, c):
        return r.at[pl.ds(mo(i * half + ls * slab, slab), slab), cols(c)]

    def remote(src, dst, ssem, rsem, dev):
        return pltpu.make_async_remote_copy(
            src_ref=src, dst_ref=dst, send_sem=ssem, recv_sem=rsem, device_id=dev, device_id_type=MESH)

    def local_copy(k, buf, r, ls, c):
        return pltpu.make_async_copy(pv(buf, ls, c), rv(r, ls, c), loc.at[k, ls * 2 * NC + c])

    def partner_copy(k, src, r, ls, c):
        q = ls * 2 * NC + c
        return remote(src, rv(r, ls, c), ps.at[k, q], pr.at[k, q], p_dev)

    def x_copy(k, src, dst, q):
        return remote(src, dst, xs.at[k, q], xr.at[k, q], x_dev)

    def y_copy(k, src, dst, q):
        return remote(src, dst, ys.at[k, q], yr.at[k, q], y_dev)

    def b_copy(r, c, slot):
        return pltpu.make_async_copy(r.at[:, cols(c)], bbuf.at[slot], bsem.at[slot])

    def compute(src, dst, ls, c, slot):
        acc = jnp.dot(panel[src, rows(ls), :], bbuf[slot], preferred_element_type=jnp.float32)
        old = panel[src, rows(ls), cols(c)].astype(jnp.float32)
        panel[dst, rows(ls), cols(c)] = jnp.minimum(acc + old, 1.0).astype(jnp.bfloat16)

    def for_each(count, body, start=0):
        def step(q, carry):
            body(q)
            return carry
        lax.fori_loop(start, count, step, 0)

    def unit_loop(count, where, r, src, dst, after):
        b_copy(r, where(0)[1], 0).start()

        def body(u):
            slot = lax.rem(u, 2)
            ls, c = where(u)

            @pl.when(u + 1 < count)
            def _():
                b_copy(r, where(u + 1)[1], 1 - slot).start()
            b_copy(r, c, slot).wait()
            compute(src, dst, ls, c, slot)
            after(u, ls, c)
        for_each(count, body)

    mine, other = j * NC, (1 - j) * NC

    barrier = pltpu.get_barrier_semaphore()
    for dev in (x_dev, y_dev, p_dev):
        pl.semaphore_signal(barrier, inc=1, device_id=dev, device_id_type=MESH)
    pl.semaphore_wait(barrier, 3)

    def own(p):
        return s_ref.at[:, cols(p)]

    def start_own(p):
        x_copy(0, own(p), pv(0, l, mine + p), p).start()
        y_copy(0, own(p), pv(0, l, mine + p), p).start()
        partner_copy(0, own(p), r0, l, mine + p).start()
    for_each(NC, start_own)
    own_load = pltpu.make_async_copy(
        s_ref, panel.at[0, rows(l), pl.ds(mo(j * half, half), half)], osem.at[0])
    own_load.start()
    own_load.wait()
    for_each(NC, lambda p: local_copy(0, 0, r0, l, mine + p).start())

    def spread(ls, c):
        local_copy(0, 0, r0, ls, c).start()
        partner_copy(0, pv(0, ls, c), r0, ls, c).start()

    def relay(p):
        x_copy(0, own(p), pv(0, l, other + p), p).wait_recv()
        spread(l, other + p)

        @pl.when(lax.rem(p, 2) == 1)
        def _():
            y_copy(0, pv(0, l, other + p), pv(0, l, other + p), NC + p // 2).start()
        y_copy(0, own(p), pv(0, 1 - l, mine + p), p).wait_recv()
        spread(1 - l, mine + p)

        @pl.when(lax.rem(p, 2) == 0)
        def _():
            x_copy(0, pv(0, 1 - l, mine + p), pv(0, 1 - l, mine + p), NC + p // 2).start()
    for_each(NC, relay)

    def diagonal(q):
        c = other + 2 * q
        x_copy(0, own(0), pv(0, 1 - l, c), NC + q).wait_recv()
        spread(1 - l, c)
        y_copy(0, own(0), pv(0, 1 - l, c + 1), NC + q).wait_recv()
        spread(1 - l, c + 1)
    for_each(NC // 2, diagonal)

    def drain(k, r):
        def body(q):
            for ls in (0, 1):
                local_copy(k, 0, r, ls, q).wait()
                partner_copy(k, pv(0, ls, q), r, ls, q).wait()
        for_each(2 * NC, body)

    def drain_sends(k, count):
        def body(q):
            x_copy(k, own(0), pv(0, 0, 0), q).wait_send()
            y_copy(k, own(0), pv(0, 0, 0), q).wait_send()
        for_each(count, body)

    def ready(k):
        for dev in (x_dev, y_dev):
            pl.semaphore_signal(rdy.at[k], inc=1, device_id=dev, device_id_type=MESH)

    drain(0, r0)
    drain_sends(0, NC + NC // 2)

    def publish(k, buf, r, ls, c):
        local_copy(k, buf, r, ls, c).start()
        partner_copy(k, pv(buf, ls, c), r, ls, c).start()

    unit_loop(4 * NC, lambda u: (lax.rem(u, 2), u // 2), r0, 0, 1,
              lambda u, ls, c: publish(1, 1, r1, ls, c))
    ready(0)
    drain(1, r1)

    def where2(u):
        first = u < NC
        second = u < 2 * NC
        third = u < 3 * NC - SHARE2
        ls = jnp.where(first | (~second & third), l, 1 - l)
        c = jnp.where(first, mine + u, jnp.where(second, other + u - NC, jnp.where(
            third, other + SHARE2 + u - 2 * NC, mine + 2 * SHARE2 + u - 3 * NC)))
        return ls, c

    def receive2(q):
        x_copy(1, own(0), pv(0, l, other + q), q).wait_recv()
        publish(2, 0, r2, l, other + q)
        y_copy(1, own(0), pv(0, 1 - l, mine + q), q).wait_recv()
        publish(2, 0, r2, 1 - l, mine + q)

    units2 = 4 * NC - 2 * SHARE2
    in_loop2 = min(SHARE2, units2 // 4 - 1)

    def after2(u, ls, c):
        publish(2, 0, r2, ls, c)

        @pl.when(u == 0)
        def _():
            pl.semaphore_wait(rdy.at[0], 2)

        @pl.when(u < SHARE2)
        def _():
            x_copy(1, pv(0, l, mine + u), pv(0, l, mine + u), u).start()
            y_copy(1, pv(0, l, mine + u), pv(0, l, mine + u), u).start()

        @pl.when((lax.rem(u, 4) == 3) & (u >= 4) & (u // 4 - 1 < in_loop2))
        def _():
            receive2(u // 4 - 1)

    unit_loop(units2, where2, r1, 1, 0, after2)
    for_each(SHARE2, receive2, start=in_loop2)
    ready(1)
    drain(2, r2)
    drain_sends(1, SHARE2)

    def where3(u):
        first = u < NC
        second = u < 2 * NC - SHARE3
        ls = jnp.where(second, l, 1 - l)
        c = jnp.where(first, mine + u, jnp.where(second, other + SHARE3 + u - NC, mine + 2 * SHARE3 + u - 2 * NC))
        return ls, c

    def receive3(q):
        y_copy(2, own(0), rv(r3, 1 - l, mine + q), q).wait_recv()
        partner_copy(3, rv(r3, 1 - l, mine + q), r3, 1 - l, mine + q).start()

    units3 = 3 * NC - 2 * SHARE3
    in_loop3 = min(SHARE3, units3 // 4 - 1)

    def after3(u, ls, c):
        @pl.when((u < NC) | (u >= 2 * NC - SHARE3))
        def _():
            publish(3, 1, r3, ls, c)

        @pl.when(u == 0)
        def _():
            pl.semaphore_wait(rdy.at[1], 2)

        @pl.when(u < SHARE3)
        def _():
            x_copy(2, pv(1, l, mine + u), pv(1, l, mine + u), u).start()
            y_copy(2, pv(1, l, mine + u), rv(r3, l, mine + u), u).start()

        @pl.when((lax.rem(u, 4) == 3) & (u >= 4) & (u // 4 - 1 < in_loop3))
        def _():
            receive3(u // 4 - 1)

    unit_loop(units3, where3, r2, 0, 1, after3)
    for_each(SHARE3, receive3, start=in_loop3)

    def drain3(q):
        local_copy(3, 1, r3, l, mine + q).wait()
        partner_copy(3, pv(1, l, mine + q), r3, l, mine + q).wait()
        partner_copy(3, pv(1, 1 - l, mine + q), r3, 1 - l, mine + q).wait()
    for_each(NC, drain3)
    for_each(NC, lambda q: local_copy(3, 1, r3, 1 - l, mine + q).wait(), start=SHARE3)
    for_each(SHARE3, lambda q: x_copy(2, own(0), pv(1, l, other + q), q).wait_recv())
    drain_sends(2, SHARE3)

    def out_copy(u, slot):
        return pltpu.make_async_copy(pv(0, l, mine + u), o_ref.at[:, cols(u)], osem.at[slot])

    def after4(u, ls, c):
        @pl.when(u > 0)
        def _():
            out_copy(u - 1, 0).wait()
        out_copy(u, 0).start()

    unit_loop(NC, lambda u: (l, mine + u), r3, 1, 0, after4)
    out_copy(NC - 1, 0).wait()


def solution(mesh):
    layout = P(('row', 'depth'), 'col')

    def step(block):
        slab, half = block.shape
        n = 2 * half
        dma = pltpu.SemaphoreType.DMA
        whole = jax.ShapeDtypeStruct((n, n), block.dtype)
        hbm = pl.BlockSpec(memory_space=pltpu.HBM)
        return pl.pallas_call(
            functools.partial(kernel, n),
            out_shape=(jax.ShapeDtypeStruct(block.shape, block.dtype),) + (whole,) * 4,
            in_specs=[hbm],
            out_specs=(hbm,) * 5,
            scratch_shapes=[
                pltpu.VMEM((2, half, n), block.dtype),
                pltpu.VMEM((2, n, n // (2 * NC)), block.dtype),
                dma((4, 4 * NC)), dma((4, 4 * NC)), dma((4, 4 * NC)),
                dma((3, NC + NC // 2)), dma((3, NC + NC // 2)),
                dma((3, NC + NC // 2)), dma((3, NC + NC // 2)),
                dma((2,)), dma((2,)), pltpu.SemaphoreType.REGULAR((2,)),
            ],
            compiler_params=pltpu.CompilerParams(
                collective_id=0, has_side_effects=True, vmem_limit_bytes=67043328),
            name='squarings',
        )(block)[0]

    return jax.shard_map(step, mesh=mesh, in_specs=(layout,), out_specs=layout, check_vma=False)
```

time: 2630 us -> 604 us (0.23); the launches traced: 2600 us -> 604 us
  waiting for transfers between devices: 1970 us -> 0 us
  Pallas kernels: 0 us -> 598 us
  starting transfers between devices: 420 us -> 0 us
  matrix products: 157 us -> 0 us
  other arithmetic: 41.5 us -> 0 us
    reduce_scatter x4 -> x0, waiting for transfers between devices: 1340 us -> none  [local_squarings(): lax.psum_scatter(partial_sum, 'depth', scatter_dimension=0, tiled=True)]
    all_gather x4 -> x0, waiting for transfers between devices: 630 us -> none  [local_squarings(): full_block = lax.all_gather(row_slab, 'depth', axis=0, tiled=True)]
    pallas_call x0 -> x1, Pallas kernels: none -> 598 us  [step(): pl.pallas_call(functools.partial(kernel, n), out_shape=(jax.ShapeDtypeStr...]
    ppermute x8 -> x0, starting transfers between devices: 420 us -> none  [the longest x4 399 us: local_squarings(): window.append(lax.ppermute(a_piece, all_axes, a_perms[piece_id]))]
    dot_general x4 -> x0, matrix products: 157 us -> none  [local_squarings(): jnp.dot(window[slot_id], b_block, preferred_element_type=jnp.float32)]
    convert_element_type x4 -> x0, other arithmetic: 41.5 us -> none  [local_squarings(): jnp.minimum(reduced + row_slab.astype(jnp.float32), 1.0)]
  transfers between devices with their start and end apart: 16 -> 0, of which waited for: 8 -> 0; matrix products, arithmetic and copies ran while one was open for 0% -> 0% of each run, Pallas kernels for 0% -> 0%
where the time goes in v1:
time: 604 us
  Pallas kernels  598 us (99%)
  local copies, waits for them, and re-layouts  6.07 us (1%)
    pallas_call x1, Pallas kernels, step(): pl.pallas_call(functools.partial(kernel, n), out_shape=(jax.ShapeDtypeStr...  598 us

profile of v1, /device:TPU:0, one launch (start us, length us, event | category | flops | bytes accessed | tf_op | source)
XLA Modules:
  0.0 603.9 jit_solution(5189615268560680828)
XLA Ops:
  0.0 597.9 %squarings.1 = (bf16[1280,2560]{1,0:T(8,128)(2,1)}, bf16[5120,5120]{1,0:T(8,128)(2,1)}, bf16[5120,5120]{1,0:T(8,128)(2,1)}, bf16[5120,5120]{1,0:T(8,128)(2,1)}, bf16[5120,5120]{1,0:T(8,128)(2,1)}) custom-call(bf16[1280,2560]{1,0:T(8,128)(2,1)} %s_ref.1), custom_call_target="tpu_custom_call" | custom-call | tf_op jit(solution)/shard_map/squarings/pallas_call | solution.py:268
  597.9 6.1 %copy.3 = bf16[1280,2560]{1,0:T(8,128)(2,1)} copy(bf16[1280,2560]{1,0:T(8,128)(2,1)} %get-tuple-element.6) | data formatting | bytes 13107200

commit v2 on v1

v2 whole, which is shorter than its diff:
```python
import functools

import jax
import jax.numpy as jnp
from jax import lax
from jax.experimental import pallas as pl
from jax.experimental.pallas import tpu as pltpu
from jax.sharding import PartitionSpec as P

MESH = pl.DeviceIdType.MESH
NC = 10
NW = 5
SHARE2 = 6
SHARE3 = 5


def kernel(n, s_ref, o_ref, r0, r1, r2, r3, p0, p1, bbuf, qbuf,
           loc, ps, pr, xs, xr, ys, yr, bsem, osem, rdy):
    half, slab, width = n // 2, n // 4, n // (2 * NC)
    l = lax.axis_index('depth')
    j = lax.axis_index('col')
    i = lax.axis_index('row')
    x_dev, y_dev, p_dev = {'col': 1 - j}, {'depth': 1 - l}, {'row': 1 - i}

    def mo(v, m):
        return pl.multiple_of(v, m)

    def rows(ls):
        return pl.ds(mo(ls * slab, slab), slab)

    def cols(c, w=1):
        return pl.ds(mo(c * w * width, w * width), w * width)

    def pv(buf, ls, c, w=1):
        return buf.at[rows(ls), cols(c, w)]

    def rv(r, ls, c, w=1):
        return r.at[pl.ds(mo(i * half + ls * slab, slab), slab), cols(c, w)]

    def remote(src, dst, ssem, rsem, dev):
        return pltpu.make_async_remote_copy(
            src_ref=src, dst_ref=dst, send_sem=ssem, recv_sem=rsem, device_id=dev, device_id_type=MESH)

    def local_copy(k, buf, r, ls, c, w=1):
        return pltpu.make_async_copy(pv(buf, ls, c, w), rv(r, ls, c, w), loc.at[k, ls * 2 * NC + c])

    def partner_copy(k, src, r, ls, c, w=1):
        q = ls * 2 * NC + c
        return remote(src, rv(r, ls, c, w), ps.at[k, q], pr.at[k, q], p_dev)

    def x_copy(k, src, dst, q):
        return remote(src, dst, xs.at[k, q], xr.at[k, q], x_dev)

    def y_copy(k, src, dst, q):
        return remote(src, dst, ys.at[k, q], yr.at[k, q], y_dev)

    def publish(k, buf, r, ls, c, w=1):
        local_copy(k, buf, r, ls, c, w).start()
        partner_copy(k, pv(buf, ls, c, w), r, ls, c, w).start()

    def settle(k, buf, r, ls, c, w=1):
        local_copy(k, buf, r, ls, c, w).wait()
        partner_copy(k, pv(buf, ls, c, w), r, ls, c, w).wait_recv()

    def sent(k, buf, r, ls, c, w=1):
        partner_copy(k, pv(buf, ls, c, w), r, ls, c, w).wait_send()

    def drain_sends(k, count, ref, w):
        def body(q):
            x_copy(k, pv(ref, 0, 0, w), pv(ref, 0, 0, w), q).wait_send()
            y_copy(k, pv(ref, 0, 0, w), pv(ref, 0, 0, w), q).wait_send()
        for_each(count, body)

    def ready(k):
        for dev in (x_dev, y_dev):
            pl.semaphore_signal(rdy.at[k], inc=1, device_id=dev, device_id_type=MESH)

    def for_each(count, body, start=0):
        def step(q, carry):
            body(q)
            return carry
        lax.fori_loop(start, count, step, 0)

    mine, other = j * NC, (1 - j) * NC
    mine_w, other_w = j * NW, (1 - j) * NW

    barrier = pltpu.get_barrier_semaphore()
    for dev in (x_dev, y_dev, p_dev):
        pl.semaphore_signal(barrier, inc=1, device_id=dev, device_id_type=MESH)
    pl.semaphore_wait(barrier, 3)

    def place(p):
        return jnp.where(l == 0, p, NW - 1 - p)

    def diag_order(q):
        return 2 if q == 1 else 1 if q == 0 else 0 if q == 2 else q

    def own(c, w=2):
        return s_ref.at[:, cols(c, w)]

    def start_own(p):
        near_c, far_c = place(p), NW - 1 - place(p)
        x_copy(0, own(near_c), pv(p0, l, mine_w + near_c, 2), p).start()
        y_copy(0, own(far_c), pv(p0, l, mine_w + far_c, 2), p).start()
        partner_copy(0, own(near_c), r0, l, mine_w + near_c, 2).start()
    for_each(NW, start_own)
    own_load = pltpu.make_async_copy(s_ref, p0.at[rows(l), pl.ds(mo(j * half, half), half)], osem.at[0])
    own_load.start()

    strip = slab // 10

    def merge(ls, c, mode):
        def body(q):
            rs = pl.ds(mo(ls * slab + q * strip, strip), strip)
            if mode == 'clear':
                p1[rs, cols(c, 2)] = jnp.zeros((strip, 2 * width), jnp.bfloat16)
            elif mode == 'copy':
                p1[rs, cols(c, 2)] = p0[rs, cols(c, 2)]
            else:
                p1[rs, cols(c, 2)] = jnp.maximum(p0[rs, cols(c, 2)], p1[rs, cols(c, 2)])
        for_each(10, body)

    for_each(NW, lambda p: merge(1 - l, other_w + p, 'clear'))
    own_load.wait()
    for_each(NW, lambda p: local_copy(0, p0, r0, l, mine_w + p, 2).start())
    for_each(NW, lambda p: merge(l, mine_w + p, 'copy'))
    for_each(NW, lambda p: settle(0, p0, r0, l, mine_w + p, 2))

    def inner(ks):
        return pl.ds(mo(ks * slab, slab), slab)

    def q_copy(ks, c, slot):
        return pltpu.make_async_copy(r0.at[inner(ks), cols(c, 2)], qbuf.at[slot], bsem.at[slot])

    def partial_loop(segments, gate, gate_fn, after=None):
        total = sum(seg[0] for seg in segments)

        def where(v):
            found, start = None, 0
            for count, ls, ks, first in segments:
                here = (ls, ks, first + (v - start) * (1 - 2 * l))
                if found is None:
                    found = here
                else:
                    later = v >= start
                    found = tuple(jnp.where(later, new, old) for new, old in zip(here, found))
                start = start + count
            return found

        @pl.when(gate == 0)
        def _():
            gate_fn()
        begin = where(jnp.int32(0))
        q_copy(begin[1], begin[2], 0).start()

        def step(v, carry):
            ls, ks, c = carry
            slot = lax.rem(v, 2)
            following = where(v + 1)

            @pl.when(v + 1 == gate)
            def _():
                gate_fn()

            @pl.when(v + 1 < total)
            def _():
                q_copy(following[1], following[2], 1 - slot).start()
            q_copy(ks, c, slot).wait()
            acc = jnp.dot(p0[rows(ls), inner(ks)], qbuf[slot], preferred_element_type=jnp.float32)
            acc = acc + p1[rows(ls), cols(c, 2)].astype(jnp.float32)
            p1[rows(ls), cols(c, 2)] = jnp.minimum(acc, 1.0).astype(jnp.bfloat16)
            if after is not None:
                after(v, ls, c)
            return following
        lax.fori_loop(0, total, step, begin)

    def flag(condition):
        return condition.astype(jnp.int32)

    ja, jb, oa, ob = 2 * j + l, 2 * j + 1 - l, 2 * (1 - j) + l, 2 * (1 - j) + 1 - l
    near, far = l, 1 - l

    def relay(q):
        a = diag_order(q)
        x_c = place(a)
        y_c = NW - 1 - x_c
        x_src = p0.at[rows(1 - l), cols(2 * (mine_w + x_c))]
        y_src = p0.at[rows(l), cols(2 * (other_w + y_c) + 1)]
        x_copy(0, x_src, x_src, NW + q).start()
        y_copy(0, y_src, y_src, NW + q).start()

    def arrive(p):
        x_c, y_c = other_w + place(p), mine_w + place(p)
        x_copy(0, own(0), pv(p0, l, x_c, 2), p).wait_recv()
        publish(0, p0, r0, l, x_c, 2)
        y_copy(0, own(0), pv(p0, 1 - l, y_c, 2), p).wait_recv()
        publish(0, p0, r0, 1 - l, y_c, 2)

        @pl.when(p == 3)
        def _():
            relay(0)
            relay(1)

        @pl.when(p == 4)
        def _():
            relay(2)
            relay(3)
            relay(4)
        merge(l, x_c, 'copy')
        merge(1 - l, y_c, 'copy')

        def gate_fn():
            settle(0, p0, r0, l, x_c, 2)
            settle(0, p0, r0, 1 - l, y_c, 2)
        at_0, at_2, at_4, from_3 = flag(p == 0), flag(p == 2), flag(p == 4), flag(p > 2)
        some, first = 3 * at_2 + from_3, place(p * from_3)
        partial_loop([
            (5 * at_0, near, ja, mine_w + place(0)),
            (4 * at_4, near, ob, mine_w + place(0)),
            (1, near, ja, x_c),
            (1, near, jb, y_c),
            (5 * at_2, near, oa, mine_w + place(0)),
            (some, near, oa, other_w + first),
            (some, far, ja, mine_w + first),
            (some, far, ja, other_w + first),
            (at_4, near, ob, mine_w + place(4)),
        ], 5 * at_0 + 4 * at_4, gate_fn)
    for_each(NW, arrive)
    for_each(NW, lambda q: publish(1, p1, r1, l, mine_w + q, 2))

    def diagonal(q):
        a = jnp.where(q == 0, 1, jnp.where(q == 1, 2, jnp.where(q == 2, 0, q)))
        d = other_w + place(a)
        x_copy(0, own(0, 1), p0.at[rows(1 - l), cols(2 * d)], NW + q).wait_recv()
        y_copy(0, own(0, 1), p0.at[rows(1 - l), cols(2 * d + 1)], NW + q).wait_recv()
        publish(0, p0, r0, 1 - l, d, 2)
        merge(1 - l, d, 'max')
        at_0, at_2, at_3, at_4 = flag(q == 0), flag(q == 2), flag(q == 3), flag(q == 4)
        fill = 5 * (at_0 + at_2 + at_3 + at_4)

        def after(v, ls, c):
            @pl.when((v == fill + 1) | ((q == 4) & ((v < fill) | (v >= fill + 3))))
            def _():
                publish(1, p1, r1, ls, c, 2)
        partial_loop([
            (5 * at_0, far, jb, mine_w + place(0)),
            (5 * at_2, far, oa, mine_w + place(0)),
            (5 * at_3, far, oa, other_w + place(0)),
            (5 * at_4, far, ob, mine_w + place(0)),
            (1, near, jb, d),
            (1, near, ob, d),
            (1, far, jb, d),
            (5 * at_4, far, ob, other_w + place(0)),
        ], fill, lambda: settle(0, p0, r0, 1 - l, d, 2), after)
    for_each(NW, diagonal)

    def flush0(q):
        sent(0, p0, r0, 0, q, 2)
        sent(0, p0, r0, 1, q, 2)
    for_each(2 * NW, flush0)
    drain_sends(0, NW, p0, 2)

    def flush_relays(q):
        x_copy(0, pv(p0, 0, 0), pv(p0, 0, 0), NW + q).wait_send()
        y_copy(0, pv(p0, 0, 0), pv(p0, 0, 0), NW + q).wait_send()
    for_each(NW, flush_relays)
    ready(0)

    def unit_loop(count, where, r, src, dst, before, after):
        def b_copy(c, slot):
            return pltpu.make_async_copy(r.at[:, cols(c)], bbuf.at[slot], bsem.at[slot])

        before(jnp.int32(0))
        b_copy(where(0)[1], 0).start()

        def body(u):
            slot = lax.rem(u, 2)
            ls, c = where(u)

            @pl.when(u + 1 < count)
            def _():
                before(u + 1)
                b_copy(where(u + 1)[1], 1 - slot).start()
            b_copy(c, slot).wait()
            acc = jnp.dot(src[rows(ls), :], bbuf[slot], preferred_element_type=jnp.float32)
            old = src[rows(ls), cols(c)].astype(jnp.float32)
            dst[rows(ls), cols(c)] = jnp.minimum(acc + old, 1.0).astype(jnp.bfloat16)
            after(u, ls, c)
        for_each(count, body)

    def where2(u):
        first = u < NC
        second = u < 2 * NC
        third = u < 3 * NC - SHARE2
        ls = jnp.where(first | (~second & third), l, 1 - l)
        c = jnp.where(first, mine + u, jnp.where(second, other + u - NC, jnp.where(
            third, other + SHARE2 + u - 2 * NC, mine + 2 * SHARE2 + u - 3 * NC)))
        return ls, c

    def before2(u):
        @pl.when((u < 2 * NC) & (lax.rem(u, 2) == 0))
        def _():
            c = jnp.where(u < NC, mine_w + u // 2, other_w + u // 2 - NW)
            for ls in (0, 1):
                settle(1, p1, r1, ls, c, 2)

    def receive2(q):
        x_copy(1, pv(p0, l, mine), pv(p0, l, other + q), q).wait_recv()
        publish(2, p0, r2, l, other + q)
        y_copy(1, pv(p0, l, mine), pv(p0, 1 - l, mine + q), q).wait_recv()
        publish(2, p0, r2, 1 - l, mine + q)

    units2 = 4 * NC - 2 * SHARE2
    in_loop2 = min(SHARE2, units2 // 4 - 1)

    def after2(u, ls, c):
        publish(2, p0, r2, ls, c)

        @pl.when(u == 0)
        def _():
            pl.semaphore_wait(rdy.at[0], 2)

        @pl.when(u < SHARE2)
        def _():
            x_copy(1, pv(p0, l, mine + u), pv(p0, l, mine + u), u).start()
            y_copy(1, pv(p0, l, mine + u), pv(p0, l, mine + u), u).start()

        @pl.when((lax.rem(u, 4) == 3) & (u >= 4) & (u // 4 - 1 < in_loop2))
        def _():
            receive2(u // 4 - 1)

    unit_loop(units2, where2, r1, p1, p0, before2, after2)
    for_each(SHARE2, receive2, start=in_loop2)

    def flush1(q):
        sent(1, p1, r1, 0, q, 2)
        sent(1, p1, r1, 1, q, 2)
    for_each(2 * NW, flush1)
    ready(1)

    def where3(u):
        first = u < NC
        second = u < 2 * NC - SHARE3
        ls = jnp.where(second, l, 1 - l)
        c = jnp.where(first, mine + u, jnp.where(second, other + SHARE3 + u - NC, mine + 2 * SHARE3 + u - 2 * NC))
        return ls, c

    def before3(u):
        @pl.when(u < 2 * NC - SHARE3)
        def _():
            for ls in (0, 1):
                settle(2, p0, r2, ls, where3(u)[1])

    def receive3(q):
        y_copy(2, pv(p1, l, mine), rv(r3, 1 - l, mine + q), q).wait_recv()
        partner_copy(3, rv(r3, 1 - l, mine + q), r3, 1 - l, mine + q).start()

    units3 = 3 * NC - 2 * SHARE3
    in_loop3 = min(SHARE3, units3 // 4 - 1)

    def after3(u, ls, c):
        @pl.when((u < NC) | (u >= 2 * NC - SHARE3))
        def _():
            publish(3, p1, r3, ls, c)

        @pl.when(u == 0)
        def _():
            pl.semaphore_wait(rdy.at[1], 2)

        @pl.when(u < SHARE3)
        def _():
            x_copy(2, pv(p1, l, mine + u), pv(p1, l, mine + u), u).start()
            y_copy(2, pv(p1, l, mine + u), rv(r3, l, mine + u), u).start()

        @pl.when((lax.rem(u, 4) == 3) & (u >= 4) & (u // 4 - 1 < in_loop3))
        def _():
            receive3(u // 4 - 1)

    unit_loop(units3, where3, r2, p0, p1, before3, after3)
    for_each(SHARE3, receive3, start=in_loop3)
    for_each(SHARE3, lambda q: x_copy(2, pv(p1, l, mine), pv(p1, l, other + q), q).wait_recv())

    def flush2(q):
        sent(2, p0, r2, 0, q)
        sent(2, p0, r2, 1, q)
    for_each(2 * NC, flush2)
    drain_sends(1, SHARE2, p0, 1)

    def unused2(q):
        settle(2, p0, r2, 0, other + q)
        settle(2, p0, r2, 1, other + q)
    for_each(SHARE3, unused2)

    def before4(u):
        settle(3, p1, r3, l, mine + u)
        partner_copy(3, pv(p1, 1 - l, mine + u), r3, 1 - l, mine + u).wait_recv()

        @pl.when(u >= SHARE3)
        def _():
            local_copy(3, p1, r3, 1 - l, mine + u).wait()

    def out_copy(u, slot):
        return pltpu.make_async_copy(pv(p0, l, mine + u), o_ref.at[:, cols(u)], osem.at[slot])

    def after4(u, ls, c):
        @pl.when(u > 0)
        def _():
            out_copy(u - 1, 0).wait()
        out_copy(u, 0).start()

    unit_loop(NC, lambda u: (l, mine + u), r3, p1, p0, before4, after4)

    def flush3(q):
        sent(3, p1, r3, 0, mine + q)
        sent(3, p1, r3, 1, mine + q)
    for_each(NC, flush3)
    drain_sends(2, SHARE3, p1, 1)
    out_copy(NC - 1, 0).wait()


def solution(mesh):
    layout = P(('row', 'depth'), 'col')

    def step(block):
        slab, half = block.shape
        n = 2 * half
        dma = pltpu.SemaphoreType.DMA
        whole = jax.ShapeDtypeStruct((n, n), block.dtype)
        hbm = pl.BlockSpec(memory_space=pltpu.HBM)
        return pl.pallas_call(
            functools.partial(kernel, n),
            out_shape=(jax.ShapeDtypeStruct(block.shape, block.dtype),) + (whole,) * 4,
            in_specs=[hbm],
            out_specs=(hbm,) * 5,
            scratch_shapes=[
                pltpu.VMEM((half, n), block.dtype),
                pltpu.VMEM((half, n), block.dtype),
                pltpu.VMEM((2, n, n // (2 * NC)), block.dtype),
                pltpu.VMEM((2, slab, n // (2 * NW)), block.dtype),
                dma((4, 4 * NC)), dma((4, 4 * NC)), dma((4, 4 * NC)),
                dma((3, NC)), dma((3, NC)), dma((3, NC)), dma((3, NC)),
                dma((2,)), dma((2,)), pltpu.SemaphoreType.REGULAR((2,)),
            ],
            compiler_params=pltpu.CompilerParams(
                collective_id=0, has_side_effects=True, vmem_limit_bytes=67043328),
            name='squarings',
        )(block)[0]

    return jax.shard_map(step, mesh=mesh, in_specs=(layout,), out_specs=layout, check_vma=False)
```

time: 604 us -> 491 us (0.81)
  Pallas kernels: 598 us -> 484 us
    pallas_call x1, Pallas kernels: 598 us -> 484 us  [step(): pl.pallas_call(functools.partial(kernel, n), out_shape=(jax.ShapeDtypeStr...]
where the time goes in v2:
time: 491 us
  Pallas kernels  484 us (99%)
  local copies, waits for them, and re-layouts  6.07 us (1%)
    pallas_call x1, Pallas kernels, step(): pl.pallas_call(functools.partial(kernel, n), out_shape=(jax.ShapeDtypeStr...  484 us

profile of v2, /device:TPU:0, one launch (start us, length us, event | category | flops | bytes accessed | tf_op | source)
XLA Modules:
  0.0 490.6 jit_solution(13809715892257141811)
XLA Ops:
  0.0 484.5 %squarings.1 = (bf16[1280,2560]{1,0:T(8,128)(2,1)}, bf16[5120,5120]{1,0:T(8,128)(2,1)}, bf16[5120,5120]{1,0:T(8,128)(2,1)}, bf16[5120,5120]{1,0:T(8,128)(2,1)}, bf16[5120,5120]{1,0:T(8,128)(2,1)}) custom-call(bf16[1280,2560]{1,0:T(8,128)(2,1)} %s_ref.1), custom_call_target="tpu_custom_call" | custom-call | tf_op jit(solution)/shard_map/squarings/pallas_call | solution.py:430
  484.5 6.1 %copy.3 = bf16[1280,2560]{1,0:T(8,128)(2,1)} copy(bf16[1280,2560]{1,0:T(8,128)(2,1)} %get-tuple-element.6) | data formatting | bytes 13107200

commit v3 on v2

v3 whole, which is shorter than its diff:
```python
import functools

import jax
import jax.numpy as jnp
from jax import lax
from jax.experimental import pallas as pl
from jax.experimental.pallas import tpu as pltpu
from jax.sharding import PartitionSpec as P

MESH = pl.DeviceIdType.MESH
NC = 10
NW = 5
X2, Y2 = 3, 4
X3, Y3 = 2, 2
OWN3 = (0, 1, 2, 4, 3)
OWN4 = (0, 2, 3, 1, 4)


def kernel(n, s_ref, o_ref, r0, r1, r2, r3, p0, p1, bbuf,
           loc, ps, pr, xs, xr, ys, yr, bsem, osem, rdy):
    half, slab, width = n // 2, n // 4, n // (2 * NC)
    l = lax.axis_index('depth')
    j = lax.axis_index('col')
    i = lax.axis_index('row')
    x_dev, y_dev, p_dev = {'col': 1 - j}, {'depth': 1 - l}, {'row': 1 - i}

    def mo(v, m):
        return pl.multiple_of(v, m)

    def rows(ls):
        return pl.ds(mo(ls * slab, slab), slab)

    def cols(c, w=1):
        return pl.ds(mo(c * w * width, w * width), w * width)

    def pv(buf, ls, c, w=1):
        return buf.at[rows(ls), cols(c, w)]

    def rv(r, ls, c, w=1):
        return r.at[pl.ds(mo(i * half + ls * slab, slab), slab), cols(c, w)]

    def remote(src, dst, ssem, rsem, dev):
        return pltpu.make_async_remote_copy(
            src_ref=src, dst_ref=dst, send_sem=ssem, recv_sem=rsem, device_id=dev, device_id_type=MESH)

    def local_copy(k, buf, r, ls, c):
        return pltpu.make_async_copy(pv(buf, ls, c, 2), rv(r, ls, c, 2), loc.at[k, ls * 2 * NW + c])

    def partner_copy(k, src, r, ls, c):
        return remote(src, rv(r, ls, c, 2), ps.at[k], pr.at[k, ls * 2 * NW + c], p_dev)

    def x_copy(k, src, dst, q):
        return remote(src, dst, xs.at[k], xr.at[(0, NC, NC + NW)[k] + q], x_dev)

    def y_copy(k, src, dst, q):
        return remote(src, dst, ys.at[k], yr.at[(0, NC, NC + NW)[k] + q], y_dev)

    def publish(k, buf, r, ls, c):
        local_copy(k, buf, r, ls, c).start()
        partner_copy(k, pv(buf, ls, c, 2), r, ls, c).start()

    def settle(k, buf, r, ls, c):
        local_copy(k, buf, r, ls, c).wait()
        partner_copy(k, pv(buf, ls, c, 2), r, ls, c).wait_recv()

    def partner_sent(k, buf, count):
        part = buf.at[:, pl.ds(0, count * width)]
        remote(part, part, ps.at[k], pr.at[k, 0], p_dev).wait_send()

    def sent(copy, k, buf, count):
        part = buf.at[rows(0), pl.ds(0, count * width)]
        copy(k, part, part, 0).wait_send()

    def ready(k):
        for dev in (x_dev, y_dev):
            pl.semaphore_signal(rdy.at[k], inc=1, device_id=dev, device_id_type=MESH)

    def for_each(count, body, start=0):
        def step(q, carry):
            body(q)
            return carry
        lax.fori_loop(start, count, step, 0)

    mine, other = j * NC, (1 - j) * NC
    mine_w, other_w = j * NW, (1 - j) * NW

    barrier = pltpu.get_barrier_semaphore()
    for dev in (x_dev, y_dev, p_dev):
        pl.semaphore_signal(barrier, inc=1, device_id=dev, device_id_type=MESH)
    pl.semaphore_wait(barrier, 3)

    def place(p):
        return jnp.where(l == 0, p, NW - 1 - p)

    def diag_order(q):
        return 2 if q == 1 else 1 if q == 0 else 0 if q == 2 else q

    def own(c, w=2):
        return s_ref.at[:, cols(c, w)]

    def start_own(p):
        near_c, far_c = place(p), NW - 1 - place(p)
        x_copy(0, own(near_c), pv(p0, l, mine_w + near_c, 2), p).start()
        y_copy(0, own(far_c), pv(p0, l, mine_w + far_c, 2), p).start()
        partner_copy(0, own(near_c), r0, l, mine_w + near_c).start()
    for_each(NW, start_own)
    own_load = pltpu.make_async_copy(s_ref, p0.at[rows(l), pl.ds(mo(j * half, half), half)], osem.at[0])
    own_load.start()

    strip = slab // 10

    def merge(ls, c, mode):
        def body(q):
            rs = pl.ds(mo(ls * slab + q * strip, strip), strip)
            if mode == 'clear':
                p1[rs, cols(c, 2)] = jnp.zeros((strip, 2 * width), jnp.bfloat16)
            elif mode == 'copy':
                p1[rs, cols(c, 2)] = p0[rs, cols(c, 2)]
            else:
                p1[rs, cols(c, 2)] = jnp.maximum(p0[rs, cols(c, 2)], p1[rs, cols(c, 2)])
        for_each(10, body)

    for_each(NW, lambda p: merge(1 - l, other_w + p, 'clear'))
    own_load.wait()
    for_each(NW, lambda p: local_copy(0, p0, r0, l, mine_w + p).start())
    for_each(NW, lambda p: merge(l, mine_w + p, 'copy'))
    for_each(NW, lambda p: settle(0, p0, r0, l, mine_w + p))

    def inner(ks):
        return pl.ds(mo(ks * slab, slab), slab)

    def q_copy(ks, c, slot):
        return pltpu.make_async_copy(r0.at[inner(ks), cols(c, 2)], bbuf.at[slot, pl.ds(0, slab), :], bsem.at[slot])

    def partial_loop(segments, total, first_gated, arrive_fn, before, after=None):
        def where(v):
            found, start = None, 0
            for count, ls, ks, first, stride in segments:
                here = (ls, ks, first + (v - start) * stride)
                if found is None:
                    found = here
                else:
                    later = v >= start
                    found = tuple(jnp.where(later, new, old) for new, old in zip(here, found))
                start = start + count
            return found

        begin = where(jnp.int32(0))

        @pl.when(jnp.logical_not(first_gated))
        def _():
            q_copy(begin[1], begin[2], 0).start()
        arrive_fn()
        before(jnp.int32(0))

        @pl.when(first_gated)
        def _():
            q_copy(begin[1], begin[2], 0).start()

        def step(v, carry):
            ls, ks, c = carry
            slot = lax.rem(v, 2)
            following = where(v + 1)
            before(v + 1)

            @pl.when(v + 1 < total)
            def _():
                q_copy(following[1], following[2], 1 - slot).start()
            q_copy(ks, c, slot).wait()
            acc = jnp.dot(p0[rows(ls), inner(ks)], bbuf[slot, pl.ds(0, slab), :], preferred_element_type=jnp.float32)
            acc = acc + p1[rows(ls), cols(c, 2)].astype(jnp.float32)
            p1[rows(ls), cols(c, 2)] = jnp.minimum(acc, 1.0).astype(jnp.bfloat16)
            if after is not None:
                after(v, ls, c)
            return following
        lax.fori_loop(0, total, step, begin)

    def flag(condition):
        return condition.astype(jnp.int32)

    ja, jb, oa, ob = 2 * j + l, 2 * j + 1 - l, 2 * (1 - j) + l, 2 * (1 - j) + 1 - l
    near, far = l, 1 - l

    def relay(q):
        a = diag_order(q)
        x_c = place(a)
        y_c = NW - 1 - x_c
        x_src = p0.at[rows(1 - l), cols(2 * (mine_w + x_c))]
        y_src = p0.at[rows(l), cols(2 * (other_w + y_c) + 1)]
        x_copy(0, x_src, x_src, NW + q).start()
        y_copy(0, y_src, y_src, NW + q).start()

    def arrive(p):
        x_c, y_c = other_w + place(p), mine_w + place(p)

        def arrive_fn():
            x_copy(0, own(0), pv(p0, l, x_c, 2), p).wait_recv()
            publish(0, p0, r0, l, x_c)
            y_copy(0, own(0), pv(p0, 1 - l, y_c, 2), p).wait_recv()
            publish(0, p0, r0, 1 - l, y_c)

            @pl.when(p == 3)
            def _():
                relay(0)
                relay(1)

            @pl.when(p == 4)
            def _():
                relay(2)
                relay(3)
                relay(4)
            merge(l, x_c, 'copy')
            merge(1 - l, y_c, 'copy')

        at_0, at_2, at_4, from_3 = flag(p == 0), flag(p == 2), flag(p == 4), flag(p > 2)
        some, first, way = 3 * at_2 + from_3, place(p * from_3), 1 - 2 * l
        gate = 5 * at_0 + 4 * at_4

        def before(v):
            @pl.when(v == gate)
            def _():
                settle(0, p0, r0, l, x_c)
                settle(0, p0, r0, 1 - l, y_c)
        partial_loop([
            (5 * at_0, near, ja, mine_w, 1),
            (4 * at_4, near, ob, mine_w + place(0), way),
            (1, near, ja, x_c, 1),
            (1, near, jb, y_c, 1),
            (5 * at_2, near, oa, mine_w, 1),
            (some, near, oa, other_w + first, way),
            (some, far, ja, mine_w + first, way),
            (some, far, ja, other_w + first, way),
            (at_4, near, ob, mine_w + place(4), 1),
        ], gate + 2 + 5 * at_2 + 3 * some + at_4, gate == 0, arrive_fn, before)
    for_each(NW, arrive)
    for_each(NW, lambda q: publish(1, p1, r1, l, mine_w + q))

    def diag_column(q):
        a = jnp.where(q == 0, 1, jnp.where(q == 1, 2, jnp.where(q == 2, 0, q)))
        return other_w + place(a)

    def diag_arrive(q):
        d = diag_column(q)
        x_copy(0, own(0, 1), p0.at[rows(1 - l), cols(2 * d)], NW + q).wait_recv()
        y_copy(0, own(0, 1), p0.at[rows(1 - l), cols(2 * d + 1)], NW + q).wait_recv()
        publish(0, p0, r0, 1 - l, d)
        merge(1 - l, d, 'max')

    def d_copy(base, v, slot):
        return pltpu.make_async_copy(
            r0.at[pl.ds(mo((1 - j) * half, half), half), cols(base + v, 2)],
            bbuf.at[slot, pl.ds(0, half), :], bsem.at[slot])

    def b_copy(r, c, slot):
        return pltpu.make_async_copy(r.at[:, cols(c, 2)], bbuf.at[slot], bsem.at[slot])

    def on(v, values, body):
        hit = v == values[0]
        for value in values[1:]:
            hit = hit | (v == value)

        @pl.when(hit)
        def _():
            body()

    def before_diag(v):
        for q, arrival, reading in ((0, None, 5), (1, 4, 8), (2, 11, 16), (3, 17, 19), (4, 23, 27)):
            if arrival is not None:
                on(v, (arrival,), lambda: diag_arrive(q))
            on(v, (reading,), lambda: settle(0, p0, r0, 1 - l, diag_column(q)))

        @pl.when(v == 30)
        def _():
            for ls in (0, 1):
                settle(1, p1, r1, ls, mine_w)
            b_copy(r1, mine_w, 0).start()

    def after_diag(v, ls, c):
        on(v, (6, 9, 17, 20, 28, 22, 23, 24, 25, 26), lambda: publish(1, p1, r1, ls, c))

    def pieces(q):
        d = diag_column(q)
        return [(1, near, jb, d, 1), (1, near, ob, d, 1), (1, far, jb, d, 1)]
    partial_loop(
        [(NW, far, jb, mine_w, 1)] + pieces(0) + pieces(1) + [(NW, far, oa, mine_w, 1)]
        + pieces(2) + pieces(3) + [(NW, far, ob, mine_w, 1)] + pieces(4),
        30, jnp.bool_(False), lambda: diag_arrive(0), before_diag, after_diag)

    partner_sent(0, p0, 4 * NW)
    sent(x_copy, 0, p0, 3 * NW)
    sent(y_copy, 0, p0, 3 * NW)
    ready(0)

    def deep_loop(base, after, tail):
        span = pl.ds(mo((1 - j) * half, half), half)

        def step(v):
            slot = lax.rem(v + 1, 2)

            @pl.when(v + 1 < NW)
            def _():
                d_copy(base, v + 1, 1 - slot).start()

            @pl.when(v + 1 == NW)
            def _():
                tail()
            d_copy(base, v, slot).wait()
            c = base + v
            acc = jnp.dot(p0[rows(1 - l), span], bbuf[slot, pl.ds(0, half), :], preferred_element_type=jnp.float32)
            acc = acc + p1[rows(1 - l), cols(c, 2)].astype(jnp.float32)
            p1[rows(1 - l), cols(c, 2)] = jnp.minimum(acc, 1.0).astype(jnp.bfloat16)
            after(c)
        for_each(NW, step)

    def unit_loop(start, stop, shift, where, r, src, dst, before, after, tail):
        def body(u):
            slot = lax.rem(u + shift, 2)
            ls, c = where(u)

            @pl.when(u + 1 < stop)
            def _():
                before(u + 1)
                b_copy(r, where(u + 1)[1], 1 - slot).start()

            @pl.when(u + 1 == stop)
            def _():
                tail()
            b_copy(r, c, slot).wait()
            acc = jnp.dot(src[rows(ls), :], bbuf[slot], preferred_element_type=jnp.float32)
            old = src[rows(ls), cols(c, 2)].astype(jnp.float32)
            dst[rows(ls), cols(c, 2)] = jnp.minimum(acc + old, 1.0).astype(jnp.bfloat16)
            after(u, ls, c)
        for_each(stop, body, start=start)

    def pick(u, table):
        found = table[-1]
        for index, value in enumerate(table[:-1]):
            found = jnp.where(u == index, value, found)
        return found

    def where2(u):
        own_u, diag_u, near_u = u < NW, u < 2 * NW, u < 3 * NW - X2
        ls = jnp.where(own_u | (~diag_u & near_u), l, 1 - l)
        c = jnp.where(own_u, mine_w + u, jnp.where(diag_u, other_w + u - NW, jnp.where(
            near_u, other_w + X2 + u - 2 * NW, mine_w + Y2 + u - 3 * NW + X2)))
        return ls, c

    def before2(u):
        @pl.when(u < 2 * NW)
        def _():
            for ls in (0, 1):
                settle(1, p1, r1, ls, where2(u)[1])

    def receive2_x(q):
        x_copy(1, pv(p0, l, mine_w, 2), pv(p0, l, other_w + q, 2), q).wait_recv()
        publish(2, p0, r2, l, other_w + q)

    def receive2_y(q):
        y_copy(1, pv(p0, l, mine_w, 2), pv(p0, 1 - l, mine_w + q, 2), q).wait_recv()
        publish(2, p0, r2, 1 - l, mine_w + q)

    def after2(u, ls, c):
        publish(2, p0, r2, ls, c)

        @pl.when(u == 0)
        def _():
            pl.semaphore_wait(rdy.at[0], 2)

        for copy, share in ((x_copy, X2), (y_copy, Y2)):
            @pl.when(u < share)
            def _():
                copy(1, pv(p0, l, mine_w + u, 2), pv(p0, l, mine_w + u, 2), u).start()

        for q, when in enumerate((5, 7, 11)):
            @pl.when(u == when)
            def _():
                receive2_x(q)
                receive2_y(q)

    def where3(u):
        own_u, near_u = u < NW, u < 2 * NW - X3
        ls = jnp.where(near_u, l, 1 - l)
        c = jnp.where(own_u, mine_w + pick(u, OWN3), jnp.where(
            near_u, other_w + X3 + u - NW, mine_w + Y3 + u - 2 * NW + X3))
        return ls, c

    def before3(u):
        @pl.when(u < 2 * NW - X3)
        def _():
            for ls in (0, 1):
                settle(2, p0, r2, ls, where3(u)[1])

    def receive3(q):
        landed = rv(r3, 1 - l, mine_w + q, 2)
        y_copy(2, pv(p1, l, mine_w, 2), landed, q).wait_recv()
        partner_copy(3, landed, r3, 1 - l, mine_w + q).start()

    def after3(u, ls, c):
        @pl.when((u < NW) | (u >= 2 * NW - X3))
        def _():
            publish(3, p1, r3, ls, c)

        @pl.when(u == 0)
        def _():
            pl.semaphore_wait(rdy.at[1], 2)

        @pl.when(u < X3)
        def _():
            x_copy(2, pv(p1, l, mine_w + u, 2), pv(p1, l, mine_w + u, 2), u).start()

        @pl.when(u < Y3)
        def _():
            y_copy(2, pv(p1, l, mine_w + u, 2), rv(r3, l, mine_w + u, 2), u).start()

        @pl.when(u == 1)
        def _():
            receive2_y(3)

        @pl.when(u == 6)
        def _():
            receive3(0)

    def where4(u):
        return l, mine_w + pick(u, OWN4)

    def before4(u):
        c = where4(u)[1]
        settle(3, p1, r3, l, c)
        partner_copy(3, pv(p1, 1 - l, c, 2), r3, 1 - l, c).wait_recv()

        @pl.when(c >= mine_w + Y3)
        def _():
            local_copy(3, p1, r3, 1 - l, c).wait()

    def out_copy(u):
        c = where4(u)[1]
        return pltpu.make_async_copy(pv(p0, l, c, 2), o_ref.at[:, cols(c - mine_w, 2)], osem.at[0])

    def after4(u, ls, c):
        @pl.when(u > 0)
        def _():
            out_copy(u - 1).wait()
        out_copy(u).start()

    def read(r, where, before, u, slot):
        def start():
            before(jnp.int32(u))
            b_copy(r, where(jnp.int32(u))[1], slot).start()
        return start

    def no_tail():
        pass

    end2, end3 = 4 * NW - X2 - Y2, 3 * NW - X3 - Y3
    unit_loop(0, NW, 0, where2, r1, p1, p0, before2, after2, lambda: d_copy(other_w, 0, NW % 2).start())
    deep_loop(other_w, lambda c: publish(1, p1, r1, 1 - l, c), read(r1, where2, before2, NW, 0))
    unit_loop(NW, end2, 1, where2, r1, p1, p0, before2, after2, read(r2, where3, before3, 0, (end2 + 1) % 2))
    partner_sent(1, p1, 4 * NW)
    ready(1)
    shift3 = (end2 + 1) % 2
    unit_loop(0, end3, shift3, where3, r2, p0, p1, before3, after3, read(r3, where4, before4, 0, (end3 + shift3) % 2))
    receive3(1)
    for_each(X3, lambda q: x_copy(2, pv(p1, l, mine_w, 2), pv(p1, l, other_w + q, 2), q).wait_recv())
    partner_sent(2, p0, 4 * NW)
    sent(x_copy, 1, p0, 2 * X2)
    sent(y_copy, 1, p0, 2 * Y2)

    def unused2(q):
        settle(2, p0, r2, 0, other_w + q)
        settle(2, p0, r2, 1, other_w + q)
    for_each(X3, unused2)
    unit_loop(0, NW, (end3 + shift3) % 2, where4, r3, p1, p0, before4, after4, no_tail)
    partner_sent(3, p1, 2 * NW)
    sent(x_copy, 2, p1, 2 * X3)
    sent(y_copy, 2, p1, 2 * Y3)
    out_copy(NW - 1).wait()


def solution(mesh):
    layout = P(('row', 'depth'), 'col')

    def step(block):
        slab, half = block.shape
        n = 2 * half
        dma = pltpu.SemaphoreType.DMA
        whole = jax.ShapeDtypeStruct((n, n), block.dtype)
        hbm = pl.BlockSpec(memory_space=pltpu.HBM)
        return pl.pallas_call(
            functools.partial(kernel, n),
            out_shape=(jax.ShapeDtypeStruct(block.shape, block.dtype),) + (whole,) * 4,
            in_specs=[hbm],
            out_specs=(hbm,) * 5,
            scratch_shapes=[
                pltpu.VMEM((half, n), block.dtype),
                pltpu.VMEM((half, n), block.dtype),
                pltpu.VMEM((2, n, n // (2 * NW)), block.dtype),
                dma((4, 4 * NW)), dma((4,)), dma((4, 4 * NW)),
                dma((3,)), dma((NC + 2 * NW,)), dma((3,)), dma((NC + 2 * NW,)),
                dma((2,)), dma((1,)), pltpu.SemaphoreType.REGULAR((2,)),
            ],
            compiler_params=pltpu.CompilerParams(
                collective_id=0, has_side_effects=True, vmem_limit_bytes=67043328),
            name='squarings',
        )(block)[0]

    return jax.shard_map(step, mesh=mesh, in_specs=(layout,), out_specs=layout, check_vma=False)
```

time: 491 us -> 465 us (0.947)
  Pallas kernels: 484 us -> 459 us
    pallas_call x1, Pallas kernels: 484 us -> 459 us  [step(): pl.pallas_call(functools.partial(kernel, n), out_shape=(jax.ShapeDtypeStr...]
where the time goes in v3:
time: 465 us
  Pallas kernels  459 us (99%)
  local copies, waits for them, and re-layouts  6.07 us (1%)
    pallas_call x1, Pallas kernels, step(): pl.pallas_call(functools.partial(kernel, n), out_shape=(jax.ShapeDtypeStr...  459 us

profile of v3, /device:TPU:0, one launch (start us, length us, event | category | flops | bytes accessed | tf_op | source)
XLA Modules:
  0.0 464.7 jit_solution(17410310889723789515)
XLA Ops:
  0.0 458.6 %squarings.1 = (bf16[1280,2560]{1,0:T(8,128)(2,1)}, bf16[5120,5120]{1,0:T(8,128)(2,1)}, bf16[5120,5120]{1,0:T(8,128)(2,1)}, bf16[5120,5120]{1,0:T(8,128)(2,1)}, bf16[5120,5120]{1,0:T(8,128)(2,1)}) custom-call(bf16[1280,2560]{1,0:T(8,128)(2,1)} %s_ref.1), custom_call_target="tpu_custom_call" | custom-call | tf_op jit(solution)/shard_map/squarings/pallas_call | solution.py:488
  458.6 6.1 %copy.3 = bf16[1280,2560]{1,0:T(8,128)(2,1)} copy(bf16[1280,2560]{1,0:T(8,128)(2,1)} %get-tuple-element.6) | data formatting | bytes 13107200

commit v4 on v3

--- a/solution.py
+++ b/solution.py
@@ -13,11 +13,11 @@
 X2, Y2 = 3, 4
 X3, Y3 = 2, 2
 OWN3 = (0, 1, 2, 4, 3)
-OWN4 = (0, 2, 3, 1, 4)
+OWN4 = (0, 3, 4, 1, 2)
 
 
 def kernel(n, s_ref, o_ref, r0, r1, r2, r3, p0, p1, bbuf,
-           loc, ps, pr, xs, xr, ys, yr, bsem, osem, rdy):
+           loc, ps, pr, xs, xr, ys, yr, bsem, psem, osem, rdy):
     half, slab, width = n // 2, n // 4, n // (2 * NC)
     l = lax.axis_index('depth')
     j = lax.axis_index('col')
@@ -132,7 +132,7 @@
     def q_copy(ks, c, slot):
         return pltpu.make_async_copy(r0.at[inner(ks), cols(c, 2)], bbuf.at[slot, pl.ds(0, slab), :], bsem.at[slot])
 
-    def partial_loop(segments, total, first_gated, arrive_fn, before, after=None):
+    def unit_table(segments):
         def where(v):
             found, start = None, 0
             for count, ls, ks, first, stride in segments:
@@ -144,7 +144,10 @@
                     found = tuple(jnp.where(later, new, old) for new, old in zip(here, found))
                 start = start + count
             return found
-
+        return where
+
+    def partial_loop(segments, total, first_gated, arrive_fn, before, after=None):
+        where = unit_table(segments)
         begin = where(jnp.int32(0))
 
         @pl.when(jnp.logical_not(first_gated))
@@ -190,6 +193,17 @@
         x_copy(0, x_src, x_src, NW + q).start()
         y_copy(0, y_src, y_src, NW + q).start()
 
+    def diag_column(q):
+        a = jnp.where(q == 0, 1, jnp.where(q == 1, 2, jnp.where(q == 2, 0, q)))
+        return other_w + place(a)
+
+    def diag_arrive(q):
+        d = diag_column(q)
+        x_copy(0, own(0, 1), p0.at[rows(1 - l), cols(2 * d)], NW + q).wait_recv()
+        y_copy(0, own(0, 1), p0.at[rows(1 - l), cols(2 * d + 1)], NW + q).wait_recv()
+        publish(0, p0, r0, 1 - l, d)
+        merge(1 - l, d, 'max')
+
     def arrive(p):
         x_c, y_c = other_w + place(p), mine_w + place(p)
 
@@ -221,6 +235,16 @@
             def _():
                 settle(0, p0, r0, l, x_c)
                 settle(0, p0, r0, 1 - l, y_c)
+
+            @pl.when((p == 4) & (v == 8))
+            def _():
+                diag_arrive(0)
+        total = gate + 2 + 5 * at_2 + 3 * some + at_4
+
+        def after(v, ls, c):
+            @pl.when((p == 4) & ((v < 4) | (v == total - 1)))
+            def _():
+                publish(1, p1, r1, ls, c)
         partial_loop([
             (5 * at_0, near, ja, mine_w, 1),
             (4 * at_4, near, ob, mine_w + place(0), way),
@@ -231,20 +255,8 @@
             (some, far, ja, mine_w + first, way),
             (some, far, ja, other_w + first, way),
             (at_4, near, ob, mine_w + place(4), 1),
-        ], gate + 2 + 5 * at_2 + 3 * some + at_4, gate == 0, arrive_fn, before)
+        ], total, gate == 0, arrive_fn, before, after)
     for_each(NW, arrive)
-    for_each(NW, lambda q: publish(1, p1, r1, l, mine_w + q))
-
-    def diag_column(q):
-        a = jnp.where(q == 0, 1, jnp.where(q == 1, 2, jnp.where(q == 2, 0, q)))
-        return other_w + place(a)
-
-    def diag_arrive(q):
-        d = diag_column(q)
-        x_copy(0, own(0, 1), p0.at[rows(1 - l), cols(2 * d)], NW + q).wait_recv()
-        y_copy(0, own(0, 1), p0.at[rows(1 - l), cols(2 * d + 1)], NW + q).wait_recv()
-        publish(0, p0, r0, 1 - l, d)
-        merge(1 - l, d, 'max')
 
     def d_copy(base, v, slot):
         return pltpu.make_async_copy(
@@ -263,28 +275,67 @@
         def _():
             body()
 
-    def before_diag(v):
-        for q, arrival, reading in ((0, None, 5), (1, 4, 8), (2, 11, 16), (3, 17, 19), (4, 23, 27)):
-            if arrival is not None:
-                on(v, (arrival,), lambda: diag_arrive(q))
-            on(v, (reading,), lambda: settle(0, p0, r0, 1 - l, diag_column(q)))
-
-        @pl.when(v == 30)
-        def _():
-            for ls in (0, 1):
-                settle(1, p1, r1, ls, mine_w)
-            b_copy(r1, mine_w, 0).start()
-
-    def after_diag(v, ls, c):
-        on(v, (6, 9, 17, 20, 28, 22, 23, 24, 25, 26), lambda: publish(1, p1, r1, ls, c))
-
     def pieces(q):
         d = diag_column(q)
         return [(1, near, jb, d, 1), (1, near, ob, d, 1), (1, far, jb, d, 1)]
-    partial_loop(
+    diag_unit = unit_table(
         [(NW, far, jb, mine_w, 1)] + pieces(0) + pieces(1) + [(NW, far, oa, mine_w, 1)]
-        + pieces(2) + pieces(3) + [(NW, far, ob, mine_w, 1)] + pieces(4),
-        30, jnp.bool_(False), lambda: diag_arrive(0), before_diag, after_diag)
+        + pieces(2) + pieces(3) + [(NW, far, ob, mine_w, 1)] + pieces(4))
+    pairs = 15
+
+    def pair_copy(units, g, slot):
+        return pltpu.make_async_copy(
+            r0.at[inner(units[g][1]), cols(units[g][2], 2)],
+            bbuf.at[slot, pl.ds(g * slab, slab), :], psem.at[slot, g])
+
+    def before_diag(b):
+        for q, arrival, reading in ((0, None, 2), (1, 3, 4), (2, 6, 8), (3, 9, None), (4, 12, 13)):
+            if arrival is not None:
+                on(b, (arrival,), lambda: diag_arrive(q))
+            if reading is not None:
+                on(b, (reading,), lambda: settle(0, p0, r0, 1 - l, diag_column(q)))
+
+        @pl.when(b == pairs)
+        def _():
+            for ls in (0, 1):
+                settle(1, p1, r1, ls, mine_w)
+            b_copy(r1, mine_w, 1).start()
+
+    def pair_at(b):
+        return [diag_unit(2 * b), diag_unit(2 * b + 1)]
+
+    first_pair = pair_at(jnp.int32(0))
+    for g in (0, 1):
+        pair_copy(first_pair, g, 0).start()
+
+    def pair_step(b, carry):
+        slot = lax.rem(b, 2)
+        units = [carry[:3], carry[3:]]
+        following = pair_at(b + 1)
+        before_diag(b + 1)
+
+        @pl.when(b + 1 < pairs)
+        def _():
+            pair_copy(following, 0, 1 - slot).start()
+
+        @pl.when((b + 1 < pairs) & (b + 1 != 9))
+        def _():
+            pair_copy(following, 1, 1 - slot).start()
+        for g in (0, 1):
+            pair_copy(units, g, slot).wait()
+        for g, (ls, ks, c) in enumerate(units):
+            acc = jnp.dot(p0[rows(ls), inner(ks)], bbuf[slot, pl.ds(g * slab, slab), :],
+                          preferred_element_type=jnp.float32)
+            acc = acc + p1[rows(ls), cols(c, 2)].astype(jnp.float32)
+            p1[rows(ls), cols(c, 2)] = jnp.minimum(acc, 1.0).astype(jnp.bfloat16)
+        @pl.when(b + 1 == 9)
+        def _():
+            settle(0, p0, r0, 1 - l, diag_column(3))
+            pair_copy(following, 1, 1 - slot).start()
+        on(b, (3, 10, 11, 12, 13, 14), lambda: publish(1, p1, r1, units[0][0], units[0][2]))
+        on(b, (4, 8, 11, 12), lambda: publish(1, p1, r1, units[1][0], units[1][2]))
+        return (*following[0], *following[1])
+    lax.fori_loop(0, pairs, pair_step, (*first_pair[0], *first_pair[1]))
 
     partner_sent(0, p0, 4 * NW)
     sent(x_copy, 0, p0, 3 * NW)
@@ -295,7 +346,7 @@
         span = pl.ds(mo((1 - j) * half, half), half)
 
         def step(v):
-            slot = lax.rem(v + 1, 2)
+            slot = lax.rem(v, 2)
 
             @pl.when(v + 1 < NW)
             def _():
@@ -381,7 +432,7 @@
         own_u, near_u = u < NW, u < 2 * NW - X3
         ls = jnp.where(near_u, l, 1 - l)
         c = jnp.where(own_u, mine_w + pick(u, OWN3), jnp.where(
-            near_u, other_w + X3 + u - NW, mine_w + Y3 + u - 2 * NW + X3))
+            near_u, other_w + X3 + u - NW, mine_w + Y3 + 1 + u - 2 * NW + X3))
         return ls, c
 
     def before3(u):
@@ -389,12 +440,40 @@
         def _():
             for ls in (0, 1):
                 settle(2, p0, r2, ls, where3(u)[1])
+
+    hrows = slab // 2
+
+    def half_of(buf, base, ls, h):
+        return buf.at[pl.ds(mo(base + ls * slab + h * hrows, hrows), hrows), cols(mine_w + Y3, 2)]
+
+    def partner_half(src, h):
+        return remote(src, half_of(r3, i * half, 1 - l, h), ps.at[3], pr.at[3, (1 - l) * 2 * NW + mine_w + Y3], p_dev)
+
+    def local_half():
+        return pltpu.make_async_copy(
+            half_of(p1, 0, 1 - l, 1), half_of(r3, i * half, 1 - l, 1), loc.at[3, (1 - l) * 2 * NW + mine_w + Y3])
+
+    def y_half(ls):
+        return y_copy(2, half_of(p1, 0, l, 0), half_of(r3, i * half, ls, 0), Y3)
 
     def receive3(q):
         landed = rv(r3, 1 - l, mine_w + q, 2)
         y_copy(2, pv(p1, l, mine_w, 2), landed, q).wait_recv()
         partner_copy(3, landed, r3, 1 - l, mine_w + q).start()
 
+    def receive3_half():
+        y_half(1 - l).wait_recv()
+        partner_half(half_of(r3, i * half, 1 - l, 0), 0).start()
+
+    def half_unit(slot, tail):
+        tail()
+        b_copy(r2, mine_w + Y3, slot).wait()
+        rs, cs = pl.ds(mo((1 - l) * slab + hrows, hrows), hrows), cols(mine_w + Y3, 2)
+        acc = jnp.dot(p0[rs, :], bbuf[slot], preferred_element_type=jnp.float32)
+        p1[rs, cs] = jnp.minimum(acc + p0[rs, cs].astype(jnp.float32), 1.0).astype(jnp.bfloat16)
+        local_half().start()
+        partner_half(half_of(p1, 0, 1 - l, 1), 1).start()
+
     def after3(u, ls, c):
         @pl.when((u < NW) | (u >= 2 * NW - X3))
         def _():
@@ -411,6 +490,10 @@
         @pl.when(u < Y3)
         def _():
             y_copy(2, pv(p1, l, mine_w + u, 2), rv(r3, l, mine_w + u, 2), u).start()
+
+        @pl.when(u == Y3)
+        def _():
+            y_half(l).start()
 
         @pl.when(u == 1)
         def _():
@@ -428,7 +511,11 @@
         settle(3, p1, r3, l, c)
         partner_copy(3, pv(p1, 1 - l, c, 2), r3, 1 - l, c).wait_recv()
 
-        @pl.when(c >= mine_w + Y3)
+        @pl.when(c == mine_w + Y3)
+        def _():
+            local_half().wait()
+
+        @pl.when(c > mine_w + Y3)
         def _():
             local_copy(3, p1, r3, 1 - l, c).wait()
 
@@ -437,6 +524,10 @@
         return pltpu.make_async_copy(pv(p0, l, c, 2), o_ref.at[:, cols(c - mine_w, 2)], osem.at[0])
 
     def after4(u, ls, c):
+        @pl.when(u == 1)
+        def _():
+            receive3_half()
+
         @pl.when(u > 0)
         def _():
             out_copy(u - 1).wait()
@@ -451,14 +542,16 @@
     def no_tail():
         pass
 
-    end2, end3 = 4 * NW - X2 - Y2, 3 * NW - X3 - Y3
-    unit_loop(0, NW, 0, where2, r1, p1, p0, before2, after2, lambda: d_copy(other_w, 0, NW % 2).start())
-    deep_loop(other_w, lambda c: publish(1, p1, r1, 1 - l, c), read(r1, where2, before2, NW, 0))
-    unit_loop(NW, end2, 1, where2, r1, p1, p0, before2, after2, read(r2, where3, before3, 0, (end2 + 1) % 2))
+    end2, end3 = 4 * NW - X2 - Y2, 3 * NW - X3 - Y3 - 1
+    unit_loop(0, NW, 1, where2, r1, p1, p0, before2, after2, lambda: d_copy(other_w, 0, 0).start())
+    deep_loop(other_w, lambda c: publish(1, p1, r1, 1 - l, c), read(r1, where2, before2, NW, 1))
+    unit_loop(NW, end2, 0, where2, r1, p1, p0, before2, after2, read(r2, where3, before3, 0, end2 % 2))
     partner_sent(1, p1, 4 * NW)
     ready(1)
-    shift3 = (end2 + 1) % 2
-    unit_loop(0, end3, shift3, where3, r2, p0, p1, before3, after3, read(r3, where4, before4, 0, (end3 + shift3) % 2))
+    shift3 = end2 % 2
+    slot3 = (end3 + shift3) % 2
+    unit_loop(0, end3, shift3, where3, r2, p0, p1, before3, after3, lambda: b_copy(r2, mine_w + Y3, slot3).start())
+    half_unit(slot3, read(r3, where4, before4, 0, 1 - slot3))
     receive3(1)
     for_each(X3, lambda q: x_copy(2, pv(p1, l, mine_w, 2), pv(p1, l, other_w + q, 2), q).wait_recv())
     partner_sent(2, p0, 4 * NW)
@@ -469,10 +562,10 @@
         settle(2, p0, r2, 0, other_w + q)
         settle(2, p0, r2, 1, other_w + q)
     for_each(X3, unused2)
-    unit_loop(0, NW, (end3 + shift3) % 2, where4, r3, p1, p0, before4, after4, no_tail)
+    unit_loop(0, NW, 1 - slot3, where4, r3, p1, p0, before4, after4, no_tail)
     partner_sent(3, p1, 2 * NW)
     sent(x_copy, 2, p1, 2 * X3)
-    sent(y_copy, 2, p1, 2 * Y3)
+    sent(y_copy, 2, p1, 2 * Y3 + 1)
     out_copy(NW - 1).wait()
 
 
@@ -496,7 +589,7 @@
                 pltpu.VMEM((2, n, n // (2 * NW)), block.dtype),
                 dma((4, 4 * NW)), dma((4,)), dma((4, 4 * NW)),
                 dma((3,)), dma((NC + 2 * NW,)), dma((3,)), dma((NC + 2 * NW,)),
-                dma((2,)), dma((1,)), pltpu.SemaphoreType.REGULAR((2,)),
+                dma((2,)), dma((2, 2)), dma((1,)), pltpu.SemaphoreType.REGULAR((2,)),
             ],
             compiler_params=pltpu.CompilerParams(
                 collective_id=0, has_side_effects=True, vmem_limit_bytes=67043328),

time: 465 us -> 461 us (level)
  Pallas kernels: 459 us -> 454 us
where the time goes in v4:
time: 461 us; the launch traced here: 460 us
  Pallas kernels  454 us (98%)
  local copies, waits for them, and re-layouts  6.07 us (1%)
    pallas_call x1, Pallas kernels, step(): pl.pallas_call(functools.partial(kernel, n), out_shape=(jax.ShapeDtypeStr...  454 us

profile of v4, /device:TPU:0, one launch (start us, length us, event | category | flops | bytes accessed | tf_op | source)
XLA Modules:
  0.0 460.2 jit_solution(8731268137284429605)
XLA Ops:
  0.0 454.1 %squarings.1 = (bf16[1280,2560]{1,0:T(8,128)(2,1)}, bf16[5120,5120]{1,0:T(8,128)(2,1)}, bf16[5120,5120]{1,0:T(8,128)(2,1)}, bf16[5120,5120]{1,0:T(8,128)(2,1)}, bf16[5120,5120]{1,0:T(8,128)(2,1)}) custom-call(bf16[1280,2560]{1,0:T(8,128)(2,1)} %s_ref.1), custom_call_target="tpu_custom_call" | custom-call | tf_op jit(solution)/shard_map/squarings/pallas_call | solution.py:581
  454.1 6.1 %copy.3 = bf16[1280,2560]{1,0:T(8,128)(2,1)} copy(bf16[1280,2560]{1,0:T(8,128)(2,1)} %get-tuple-element.6) | data formatting | bytes 13107200

commit v5 on v4

--- a/solution.py
+++ b/solution.py
@@ -204,6 +204,24 @@
         publish(0, p0, r0, 1 - l, d)
         merge(1 - l, d, 'max')
 
+    def pieces(q):
+        d = diag_column(q)
+        return [(1, near, jb, d, 1), (1, near, ob, d, 1), (1, far, jb, d, 1)]
+    diag_unit = unit_table(
+        [(NW, far, jb, mine_w, 1)] + pieces(0) + pieces(1) + [(NW, far, oa, mine_w, 1)]
+        + pieces(2) + pieces(3) + [(NW, far, ob, mine_w, 1)] + pieces(4))
+    pairs = 15
+
+    def pair_copy(units, g, slot):
+        return pltpu.make_async_copy(
+            r0.at[inner(units[g][1]), cols(units[g][2], 2)],
+            bbuf.at[slot, pl.ds(g * slab, slab), :], psem.at[slot, g])
+
+    def pair_at(b):
+        return [diag_unit(2 * b), diag_unit(2 * b + 1)]
+
+    first_pair = pair_at(jnp.int32(0))
+
     def arrive(p):
         x_c, y_c = other_w + place(p), mine_w + place(p)
 
@@ -239,6 +257,11 @@
             @pl.when((p == 4) & (v == 8))
             def _():
                 diag_arrive(0)
+
+            @pl.when((p == 4) & (v == 10))
+            def _():
+                for g in (0, 1):
+                    pair_copy(first_pair, g, 0).start()
         total = gate + 2 + 5 * at_2 + 3 * some + at_4
 
         def after(v, ls, c):
@@ -275,19 +298,6 @@
         def _():
             body()
 
-    def pieces(q):
-        d = diag_column(q)
-        return [(1, near, jb, d, 1), (1, near, ob, d, 1), (1, far, jb, d, 1)]
-    diag_unit = unit_table(
-        [(NW, far, jb, mine_w, 1)] + pieces(0) + pieces(1) + [(NW, far, oa, mine_w, 1)]
-        + pieces(2) + pieces(3) + [(NW, far, ob, mine_w, 1)] + pieces(4))
-    pairs = 15
-
-    def pair_copy(units, g, slot):
-        return pltpu.make_async_copy(
-            r0.at[inner(units[g][1]), cols(units[g][2], 2)],
-            bbuf.at[slot, pl.ds(g * slab, slab), :], psem.at[slot, g])
-
     def before_diag(b):
         for q, arrival, reading in ((0, None, 2), (1, 3, 4), (2, 6, 8), (3, 9, None), (4, 12, 13)):
             if arrival is not None:
@@ -301,12 +311,6 @@
                 settle(1, p1, r1, ls, mine_w)
             b_copy(r1, mine_w, 1).start()
 
-    def pair_at(b):
-        return [diag_unit(2 * b), diag_unit(2 * b + 1)]
-
-    first_pair = pair_at(jnp.int32(0))
-    for g in (0, 1):
-        pair_copy(first_pair, g, 0).start()
 
     def pair_step(b, carry):
         slot = lax.rem(b, 2)

time: 461 us -> 460 us (level)
  no operation moved by 1% of the time
where the time goes in v5:
time: 460 us
  Pallas kernels  454 us (99%)
  local copies, waits for them, and re-layouts  6.07 us (1%)
    pallas_call x1, Pallas kernels, step(): pl.pallas_call(functools.partial(kernel, n), out_shape=(jax.ShapeDtypeStr...  454 us

profile of v5, /device:TPU:0, one launch (start us, length us, event | category | flops | bytes accessed | tf_op | source)
XLA Modules:
  0.0 460.2 jit_solution(11709051786733330058)
XLA Ops:
  0.0 454.1 %squarings.1 = (bf16[1280,2560]{1,0:T(8,128)(2,1)}, bf16[5120,5120]{1,0:T(8,128)(2,1)}, bf16[5120,5120]{1,0:T(8,128)(2,1)}, bf16[5120,5120]{1,0:T(8,128)(2,1)}, bf16[5120,5120]{1,0:T(8,128)(2,1)}) custom-call(bf16[1280,2560]{1,0:T(8,128)(2,1)} %s_ref.1), custom_call_target="tpu_custom_call" | custom-call | tf_op jit(solution)/shard_map/squarings/pallas_call | solution.py:585
  454.1 6.1 %copy.3 = bf16[1280,2560]{1,0:T(8,128)(2,1)} copy(bf16[1280,2560]{1,0:T(8,128)(2,1)} %get-tuple-element.6) | data formatting | bytes 13107200
